TPU v7x, 32 devices: a whole 2x2x4 slice. The times are simulated.
32 devices in a mesh: grp: 2 (over x), sub: 16 (over z, y, core).
Axes of the slice: x: 2, y: 2, z: 4, core: 2. Of those that a mesh axis runs over, the one named last changes fastest.
Arguments:
- counts: int32 [32], P(('grp', 'sub')), may hold values from 1 to 3, as said below
- block_map: int32 [96], P(('grp', 'sub')), may hold values from 0 to 31
- perms: int32 [96, 256], P(('grp', 'sub')), may hold values from 0 to 255, each once within a row
- mass_ii: bfloat16 [96, 1024, 1024], P(('grp', 'sub')), may hold values from -0.005859375 to 0.005859375
- mass_ib: bfloat16 [96, 1024, 256], P(('grp', 'sub')), may hold values from -0.1875 to 0.1875
- mass_bb: bfloat16 [96, 256, 256], P(('grp', 'sub')), may hold values from -6 to 6
- constraint_modes: bfloat16 [96, 1024, 256], P(('grp', 'sub')), may hold values from -6 to 6
- fixed_modes: bfloat16 [96, 1024, 128], P(('grp', 'sub')), may hold values from -6 to 6
Outputs:
- blocks: float32 [32, 256, 256], P('grp', 'sub')
- coupling: float32 [96, 128, 256], P(('grp', 'sub'))
Inputs may be any that keep to these rules, and one draw needn't show every extreme that they name: `counts`: at least one device uses all 3 slots and one uses a single slot.
All inputs are finite; a program needn't handle non-finite values.
Results may differ from a plain program's by a relative error of at most 0.0021.
Values sent between devices are 32-bit elements; how exact they have to be, the bound alone decides.
A program may use at most 128 MiB of HBM per device.

v0:
```python
import jax
import jax.numpy as jnp
from jax import lax
from jax.sharding import PartitionSpec as P

NBG = 16


def shifted(value, axis, by):
    peers = lax.axis_size(axis)
    return lax.ppermute(value, axis, [(i, (i + by) % peers) for i in range(peers)])


def contract(left, right):
    return lax.dot_general(
        left, right, (((0,), (0,)), ((), ())), preferred_element_type=jnp.float32
    )


def reduce_slot(mass_ii, mass_ib, mass_bb, constraint_modes, fixed_modes):
    product = jnp.dot(mass_ii, constraint_modes, preferred_element_type=jnp.float32).astype(
        jnp.bfloat16
    )
    cross = contract(constraint_modes, mass_ib)
    reduced = contract(constraint_modes, product) + cross + cross.T + mass_bb.astype(jnp.float32)
    coupled = contract(fixed_modes, product) + contract(fixed_modes, mass_ib)
    return (reduced, coupled)


def per_device(counts, block_map, perms, mass_ii, mass_ib, mass_bb, constraint_modes, fixed_modes):
    width = mass_bb.shape[1]
    modes = fixed_modes.shape[2]
    slot_total = mass_ii.shape[0]
    used_count = counts[0]
    sub_size = lax.axis_size("sub")

    def pick(array, slot_index):
        return lax.dynamic_index_in_dim(array, slot_index, 0, keepdims=False)

    start_parts = jnp.zeros((slot_total, width, width), jnp.float32)
    carry_state = (start_parts, jnp.zeros((slot_total, modes, width), jnp.float32))
    for slot_index in range(slot_total):
        one_parts, one_coupling = carry_state
        reduced, coupled = reduce_slot(
            pick(mass_ii, slot_index),
            pick(mass_ib, slot_index),
            pick(mass_bb, slot_index),
            pick(constraint_modes, slot_index),
            pick(fixed_modes, slot_index),
        )
        active = (slot_index < used_count).astype(jnp.float32)
        perm_row = pick(perms, slot_index)
        inverse = (
            jnp.zeros((width,), jnp.int32).at[perm_row].set(jnp.arange(width, dtype=jnp.int32))
        )
        placed = reduced[inverse][:, inverse] * active
        one_parts = lax.dynamic_update_index_in_dim(one_parts, placed, slot_index, 0)
        one_coupling = lax.dynamic_update_index_in_dim(
            one_coupling, coupled * active, slot_index, 0
        )
        carry_state = (one_parts, one_coupling)
    parts, coupling = carry_state
    slot_ids = jnp.arange(slot_total, dtype=jnp.int32)
    active_col = (slot_ids < used_count).astype(jnp.float32)
    targets = jnp.arange(2 * NBG, dtype=jnp.int32)
    one_hot = (block_map[:, None] == targets[None, :]).astype(jnp.float32) * active_col[:, None]
    spread_hot = jnp.broadcast_to(one_hot[:, None, :], (slot_total, sub_size, 2 * NBG))
    rows_in, hot_in = (
        lax.all_to_all(parts, "sub", split_axis=1, concat_axis=0, tiled=True),
        lax.all_to_all(spread_hot, "sub", split_axis=1, concat_axis=0, tiled=True),
    )
    hot_flat = hot_in[:, 0, :]
    owned = jnp.einsum("rc,rab->cab", hot_flat, rows_in, precision=lax.Precision.HIGHEST)
    home_rows = owned[:NBG]
    ahead_rows = owned[NBG:]
    blocks = home_rows + shifted(ahead_rows, "grp", 1)
    return (blocks, coupling)


def solution(mesh):
    placed = (
        P(("grp", "sub")),
        P(("grp", "sub")),
        P(("grp", "sub"), None),
        P(("grp", "sub"), None, None),
        P(("grp", "sub"), None, None),
        P(("grp", "sub"), None, None),
        P(("grp", "sub"), None, None),
        P(("grp", "sub"), None, None),
    )
    return jax.shard_map(
        per_device,
        mesh=mesh,
        in_specs=placed,
        out_specs=(P("grp", "sub", None), P(("grp", "sub"), None, None)),
        check_vma=False,
    )
```

profile of v0, /device:TPU:0, one launch (start us, length us, event | category | flops | bytes accessed | tf_op | source)
XLA Modules:
  0.0 96.1 jit_solution(16782596118019003462)
XLA Ops:
  0.6 0.0 copy-start
  1.4 0.7 fusion.83
  2.1 0.6 broadcast_in_dim.40
  2.8 7.5 %all-to-all-start = ((f32[3,16,32]{2,0,1:T(4,128)}), f32[3,16,32]{2,0,1:T(4,128)}, u32[]{:S(2)}, u32[]{:S(2)}) async-start(f32[3,16,32]{2,0,1:T(4,128)} %broadcast_in_dim.40), calls=%async_computation | async-start | bytes 65536 | tf_op jit(solution)/shard_map/all_to_all | solution.py:70
  10.2 2.2 %fusion.50 = f32[256,256]{1,0:T(8,128)} fusion(bf16[3,1024,256]{2,1,0:T(8,128)(2,1)} %param.12, bf16[3,1024,256]{2,1,0:T(8,128)(2,1)} %param.14), kind=kOutput, calls=%fused_computation.62 | convolution fusion | flops 134217728 | bytes 1310720 | tf_op jit(solution)/shard_map/dot_general | solution.py:15
  12.5 2.1 %fusion.38 = f32[256,256]{1,0:T(8,128)} fusion(bf16[3,1024,256]{2,1,0:T(8,128)(2,1)} %param.12, bf16[3,1024,256]{2,1,0:T(8,128)(2,1)S(1)} %copy-done), kind=kOutput, calls=%fused_computation.50 | convolution fusion | flops 134217728 | bytes 1310720 | tf_op jit(solution)/shard_map/dot_general | solution.py:15
  14.6 1.5 %fusion.44 = f32[256,256]{1,0:T(8,128)S(1)} fusion(bf16[3,1024,256]{2,1,0:T(8,128)(2,1)} %param.12, bf16[3,1024,256]{2,1,0:T(8,128)(2,1)S(1)} %copy-done), kind=kOutput, calls=%fused_computation.56 | convolution fusion | flops 134217728 | bytes 1310720 | tf_op jit(solution)/shard_map/dot_general | solution.py:15
  16.1 0.0 copy-start.3
  16.1 2.8 %fusion.9 = bf16[1024,256]{1,0:T(8,128)(2,1)S(1)} fusion(bf16[3,1024,1024]{2,1,0:T(8,128)(2,1)} %param.11, bf16[3,1024,256]{2,1,0:T(8,128)(2,1)S(1)} %copy-done), kind=kOutput, calls=%fused_computation.18 | convolution fusion | flops 537133056 | bytes 3145728 | tf_op jit(solution)/shard_map/dot_general | solution.py:21
  18.9 0.7 fusion.15
  19.6 0.0 copy-start.9
  19.6 0.7 fusion.12
  20.4 1.4 %scatter_custom_fusion = s32[256]{0:T(256)S(1)} fusion(s32[256]{0:T(256)S(1)} %bitcast.172, s32[256]{0:T(256)S(1)} %iota.22, s32[]{:T(128)} %constant.74.clone.1), kind=kCustom, calls=%fused_computation.115 | custom fusion | bytes 1028 | tf_op jit(solution)/shard_map/scatter | solution.py:54
  21.8 1.4 %scatter_custom_fusion.1 = s32[256]{0:T(256)S(1)} fusion(s32[256]{0:T(256)S(1)} %bitcast.171, s32[256]{0:T(256)S(1)} %iota.23, s32[]{:T(128)} %constant.74.clone.1), kind=kCustom, calls=%fused_computation.113 | custom fusion | bytes 1028 | tf_op jit(solution)/shard_map/scatter | solution.py:54
  23.2 1.4 %scatter_custom_fusion.2 = s32[256]{0:T(256)S(1)} fusion(s32[256]{0:T(256)S(1)} %bitcast.170, s32[256]{0:T(256)S(1)} %iota.24, s32[]{:T(128)} %constant.74.clone.1), kind=kCustom, calls=%fused_computation.111 | custom fusion | bytes 1028 | tf_op jit(solution)/shard_map/scatter | solution.py:54
  24.7 0.0 copy-done.3
  24.7 0.8 copy.53
  25.5 1.8 %copy.57 = f32[256,256]{0,1:T(8,128)} copy(f32[256,256]{1,0:T(8,128)} %fusion.38) | data formatting | bytes 524288 | tf_op jit(solution)/shard_map/dot_general | solution.py:15
  27.4 1.8 %copy.49 = f32[256,256]{0,1:T(8,128)} copy(f32[256,256]{1,0:T(8,128)} %fusion.50) | data formatting | bytes 524288 | tf_op jit(solution)/shard_map/dot_general | solution.py:15
  29.2 1.7 %fusion.90 = (bf16[1,256,256]{2,1,0:T(8,128)(2,1)}, bf16[1,256,256]{2,1,0:T(8,128)(2,1)}, bf16[1,256,256]{2,1,0:T(8,128)(2,1)S(1)}) fusion(bf16[3,256,256]{2,1,0:T(8,128)(2,1)} %param.13), kind=kLoop, calls=%fused_computation.117 | loop fusion | bytes 786432 | tf_op jit(solution)/shard_map/jit(dynamic_index_in_dim)/dynamic_slice | solution.py:38
  30.9 1.7 %copy.78 = bf16[1,256,256]{1,2,0:T(8,128)(2,1)} copy(bf16[1,256,256]{2,1,0:T(8,128)(2,1)} %get-tuple-element.8) | data formatting | bytes 262144
  32.6 1.7 %copy.77 = bf16[1,256,256]{1,2,0:T(8,128)(2,1)} copy(bf16[1,256,256]{2,1,0:T(8,128)(2,1)} %get-tuple-element.9) | data formatting | bytes 262144
  34.2 0.7 copy.76
  35.0 2.0 %fusion.26 = f32[256,256]{0,1:T(8,128)} fusion(f32[256,256]{0,1:T(8,128)} %copy.49, bf16[1024,256]{1,0:T(8,128)(2,1)S(1)} %fusion.9, bf16[3,1024,256]{2,1,0:T(8,128)(2,1)S(1)} %copy-done, f32[256,256]{1,0:T(8,128)S(1)} %copy-done.4, bf16[1,256,256]{1,2,0:T(8,128)(2,1)} %copy.76), kind=kOutput, calls=%fused_computation.32 | convolution fusion | flops 134479872 | bytes 1966080 | tf_op jit(solution)/shard_map/dot_general | solution.py:15
  37.0 1.1 %copy.51 = f32[256,256]{1,0:T(8,128)S(1)} copy(f32[256,256]{0,1:T(8,128)} %fusion.26) | data formatting | bytes 524288 | tf_op jit(solution)/shard_map/add | solution.py:25
  38.1 1.7 %gather_fusion = f32[256,256]{1,0:T(8,128)} fusion(f32[256,256]{1,0:T(8,128)S(1)} %copy.51, s32[1024]{0:T(1024)S(1)} %pad_clamp_fusion.2), kind=kCustom, calls=%fused_computation | custom fusion | bytes 525312 | tf_op jit(solution)/shard_map/gather | solution.py:56
  39.7 1.1 %copy.52 = f32[256,256]{0,1:T(8,128)S(1)} copy(f32[256,256]{1,0:T(8,128)} %gather_fusion) | data formatting | bytes 524288 | tf_op jit(solution)/shard_map/gather | solution.py:56
  40.9 1.7 %gather_fusion.1 = f32[256,256]{1,0:T(8,128)} fusion(f32[256,256]{0,1:T(8,128)S(1)} %copy.52, s32[1024]{0:T(1024)S(1)} %pad_clamp_fusion.2), kind=kCustom, calls=%fused_computation.1 | custom fusion | bytes 525312 | tf_op jit(solution)/shard_map/gather | solution.py:56
  42.5 2.1 %fusion.22 = f32[256,256]{0,1:T(8,128)} fusion(f32[256,256]{0,1:T(8,128)} %copy.57, bf16[1024,256]{1,0:T(8,128)(2,1)S(1)} %fusion.15, bf16[3,1024,256]{2,1,0:T(8,128)(2,1)S(1)} %copy-done, f32[256,256]{1,0:T(8,128)} %fusion.38, bf16[1,256,256]{1,2,0:T(8,128)(2,1)S(1)} %copy-done.8), kind=kOutput, calls=%fused_computation.28 | convolution fusion | flops 134479872 | bytes 1966080 | tf_op jit(solution)/shard_map/dot_general | solution.py:15
  44.6 1.1 %copy.59 = f32[256,256]{1,0:T(8,128)S(1)} copy(f32[256,256]{0,1:T(8,128)} %fusion.22) | data formatting | bytes 524288 | tf_op jit(solution)/shard_map/add | solution.py:25
  45.7 1.7 %gather_fusion.4 = f32[256,256]{1,0:T(8,128)} fusion(f32[256,256]{1,0:T(8,128)S(1)} %copy.59, s32[1024]{0:T(1024)S(1)} %pad_clamp_fusion), kind=kCustom, calls=%fused_computation.4 | custom fusion | bytes 525312 | tf_op jit(solution)/shard_map/gather | solution.py:56
  47.3 1.1 %copy.60 = f32[256,256]{0,1:T(8,128)S(1)} copy(f32[256,256]{1,0:T(8,128)} %gather_fusion.4) | data formatting | bytes 524288 | tf_op jit(solution)/shard_map/gather | solution.py:56
  48.5 1.7 %gather_fusion.5 = f32[256,256]{1,0:T(8,128)} fusion(f32[256,256]{0,1:T(8,128)S(1)} %copy.60, s32[1024]{0:T(1024)S(1)} %pad_clamp_fusion), kind=kCustom, calls=%fused_computation.5 | custom fusion | bytes 525312 | tf_op jit(solution)/shard_map/gather | solution.py:56
  50.1 1.4 %fusion.24 = f32[256,256]{0,1:T(8,128)S(1)} fusion(f32[256,256]{0,1:T(8,128)} %copy.53, bf16[1024,256]{1,0:T(8,128)(2,1)S(1)} %fusion.12, bf16[3,1024,256]{2,1,0:T(8,128)(2,1)S(1)} %copy-done, f32[256,256]{1,0:T(8,128)} %copy-done.3, bf16[1,256,256]{1,2,0:T(8,128)(2,1)S(1)} %copy-done.7), kind=kOutput, calls=%fused_computation.30 | convolution fusion | flops 134479872 | bytes 1966080 | tf_op jit(solution)/shard_map/dot_general | solution.py:15
  51.5 0.1 copy.55
  51.6 1.0 %gather_fusion.2 = f32[256,256]{1,0:T(8,128)S(1)} fusion(f32[256,256]{1,0:T(8,128)S(1)} %copy.55, s32[1024]{0:T(1024)S(1)} %pad_clamp_fusion.1), kind=kCustom, calls=%fused_computation.2 | custom fusion | bytes 525312 | tf_op jit(solution)/shard_map/gather | solution.py:56
  52.6 0.0 copy-start.1
  52.6 0.1 copy.56
  52.8 1.0 %gather_fusion.3 = f32[256,256]{1,0:T(8,128)S(1)} fusion(f32[256,256]{0,1:T(8,128)S(1)} %copy.56, s32[1024]{0:T(1024)S(1)} %pad_clamp_fusion.1), kind=kCustom, calls=%fused_computation.3 | custom fusion | bytes 525312 | tf_op jit(solution)/shard_map/gather | solution.py:56
  53.7 0.0 copy-done.1
  53.8 0.0 copy-start.2
  53.8 0.1 dynamic_update_slice.20
  53.9 0.8 copy-done.2
  54.7 1.3 %copy.61 = f32[3,256,256]{2,0,1:T(4,128)} copy(f32[3,256,256]{1,2,0:T(8,128)S(1)} %bitcast_dynamic-update-slice_fusion) | data formatting | bytes 1572864 | tf_op jit(solution)/shard_map/jit(dynamic_update_index_in_dim)/dynamic_update_slice | solution.py:57
  56.0 0.0 all-to-all-done
  56.0 6.0 %all-to-all-start.1 = ((f32[3,256,256]{2,0,1:T(4,128)}), f32[3,256,256]{2,0,1:T(4,128)S(1)}, u32[]{:S(2)}, u32[]{:S(2)}) async-start(f32[3,256,256]{2,0,1:T(4,128)} %copy.61), calls=%async_computation.1 | async-start | bytes 2097152 | tf_op jit(solution)/shard_map/all_to_all | solution.py:69
  62.0 0.0 copy-start.5
  62.0 1.4 %convolution_bitcast_fusion.5 = f32[128,256]{0,1:T(8,128)S(1)} fusion(bf16[1024,256]{1,0:T(8,128)(2,1)S(1)} %fusion.9, bf16[3,1024,128]{2,1,0:T(8,128)(2,1)} %param.15), kind=kOutput, calls=%fused_computation.46 | convolution fusion | flops 67108864 | bytes 917504 | tf_op jit(solution)/shard_map/dot_general | solution.py:15
  63.4 1.5 %fusion.34 = f32[1,128,256]{1,2,0:T(8,128)S(1)} fusion(f32[128,256]{0,1:T(8,128)S(1)} %convolution_bitcast_fusion.5, bf16[3,1024,256]{2,1,0:T(8,128)(2,1)} %param.12, bf16[3,1024,128]{2,1,0:T(8,128)(2,1)} %param.15, f32[]{:T(128)S(6)} %convert_element_type.48), kind=kOutput, calls=%fused_computation.45 | convolution fusion | flops 67174400 | bytes 1048580 | tf_op jit(solution)/shard_map/dot_general | solution.py:15
  64.9 0.3 convolution_bitcast_fusion.4
  65.2 1.4 %fusion.32 = f32[3,128,256]{1,2,0:T(8,128)S(1)} fusion(f32[3,128,256]{1,2,0:T(8,128)S(1)} %dynamic_update_slice.23, f32[128,256]{0,1:T(8,128)S(1)} %convolution_bitcast_fusion.4, bf16[3,1024,256]{2,1,0:T(8,128)(2,1)} %param.12, bf16[3,1024,128]{2,1,0:T(8,128)(2,1)S(1)} %copy-done.5, f32[]{:T(128)S(6)} %convert_element_type.52), kind=kOutput, calls=%fused_computation.41 | convolution fusion | flops 67174400 | bytes 1048580 | tf_op jit(solution)/shard_map/dot_general | solution.py:15
  66.6 0.8 squeeze.60
  67.4 17.5 %all-to-all-done.1 = f32[3,256,256]{2,0,1:T(4,128)S(1)} async-done(((f32[3,256,256]{2,0,1:T(4,128)}), f32[3,256,256]{2,0,1:T(4,128)S(1)}, u32[]{:S(2)}, u32[]{:S(2)}) %all-to-all-start.1) | async-done | bytes 786464 | tf_op jit(solution)/shard_map/all_to_all | solution.py:69
  84.9 0.2 copy.62
  85.0 0.0 copy-start.6
  85.1 0.1 copy.63
  85.1 1.0 %fusion.35 = f32[32,16,256]{2,0,1:T(8,128)S(1)} fusion(f32[48,16,256]{2,1,0:T(8,128)S(1)} %bitcast.169, f32[48,32]{1,0:T(8,128)S(1)} %squeeze.60), kind=kOutput, calls=%fused_computation.47 | convolution fusion | flops 75497472 | bytes 1316864 | tf_op jit(solution)/shard_map/rc,rab->cab/dot_general | solution.py:73
  86.2 1.6 %collective-permute-start = (f32[16,16,256]{2,0,1:T(8,128)S(1)}, f32[16,16,256]{2,0,1:T(8,128)S(1)}, u32[]{:S(2)}, u32[]{:S(2)}) collective-permute-start(f32[16,16,256]{2,0,1:T(8,128)S(1)} %slice.39), channel_id=1, source_target_pairs={{0,16},{16,0},{1,17},{17,1},{2,18},{18,2},{3,19},{19,3},{4,20},{20... | collective-permute-start | bytes 786440 | tf_op jit(solution)/shard_map/ppermute | solution.py:11
  87.8 0.0 copy-done.6
  87.8 0.3 convolution_bitcast_fusion.3
  88.1 1.4 %fusion.29 = f32[3,128,256]{1,2,0:T(8,128)S(1)} fusion(f32[3,128,256]{1,2,0:T(8,128)S(1)} %fusion.32, f32[128,256]{0,1:T(8,128)S(1)} %convolution_bitcast_fusion.3, bf16[3,1024,256]{2,1,0:T(8,128)(2,1)} %param.12, bf16[3,1024,128]{2,1,0:T(8,128)(2,1)S(1)} %copy-done.6, f32[]{:T(128)S(6)} %convert_element_type.56), kind=kOutput, calls=%fused_computation.36 | convolution fusion | flops 67174400 | bytes 1048580 | tf_op jit(solution)/shard_map/dot_general | solution.py:15
  89.5 0.9 copy.70
  90.4 4.8 %collective-permute-done = f32[16,16,256]{2,0,1:T(8,128)S(1)} collective-permute-done((f32[16,16,256]{2,0,1:T(8,128)S(1)}, f32[16,16,256]{2,0,1:T(8,128)S(1)}, u32[]{:S(2)}, u32[]{:S(2)}) %collective-permute-start) | collective-permute-done | bytes 262176 | tf_op jit(solution)/shard_map/ppermute | solution.py:11
  95.2 0.9 copy.69
  (27 shorter events, 0.2 us)
Async XLA Ops:
  0.6 11.8 %copy-start = (bf16[3,1024,256]{2,1,0:T(8,128)(2,1)S(1)}, bf16[3,1024,256]{2,1,0:T(8,128)(2,1)}, u32[]{:S(2)}) copy-start(bf16[3,1024,256]{2,1,0:T(8,128)(2,1)} %param.14) | copy-start | bytes 4718596
  2.8 53.3 %all-to-all-start = ((f32[3,16,32]{2,0,1:T(4,128)}), f32[3,16,32]{2,0,1:T(4,128)}, u32[]{:S(2)}, u32[]{:S(2)}) async-start(f32[3,16,32]{2,0,1:T(4,128)} %broadcast_in_dim.40), calls=%async_computation | async-start | bytes 65536 | tf_op jit(solution)/shard_map/all_to_all | solution.py:70
  14.6 4.3 %copy-start.10 = (bf16[3,1024,1024]{2,1,0:T(8,128)(2,1)S(1)}, bf16[3,1024,1024]{2,1,0:T(8,128)(2,1)}, u32[]{:S(2)}) copy-start(bf16[3,1024,1024]{2,1,0:T(8,128)(2,1)} %param.11) | copy-start | bytes 18874372
  16.1 8.6 %copy-start.3 = (f32[256,256]{1,0:T(8,128)}, f32[256,256]{1,0:T(8,128)S(1)}, u32[]{:S(2)}) copy-start(f32[256,256]{1,0:T(8,128)S(1)} %fusion.44) | copy-start | bytes 786436
  19.6 0.7 copy-start.9
  25.5 9.4 %copy-start.4 = (f32[256,256]{1,0:T(8,128)S(1)}, f32[256,256]{1,0:T(8,128)}, u32[]{:S(2)}) copy-start(f32[256,256]{1,0:T(8,128)} %fusion.50) | copy-start | bytes 786436
  39.7 2.8 %copy-start.8 = (bf16[1,256,256]{1,2,0:T(8,128)(2,1)S(1)}, bf16[1,256,256]{1,2,0:T(8,128)(2,1)}, u32[]{:S(2)}) copy-start(bf16[1,256,256]{1,2,0:T(8,128)(2,1)} %copy.78) | copy-start | bytes 393220
  47.3 2.8 %copy-start.7 = (bf16[1,256,256]{1,2,0:T(8,128)(2,1)S(1)}, bf16[1,256,256]{1,2,0:T(8,128)(2,1)}, u32[]{:S(2)}) copy-start(bf16[1,256,256]{1,2,0:T(8,128)(2,1)} %copy.77) | copy-start | bytes 393220
  52.6 1.1 %copy-start.1 = (f32[256,256]{1,0:T(8,128)S(1)}, f32[256,256]{1,0:T(8,128)}, u32[]{:S(2)}) copy-start(f32[256,256]{1,0:T(8,128)} %gather_fusion.1) | copy-start | bytes 786436
  53.8 1.0 copy-start.2
  56.0 28.8 %all-to-all-start.1 = ((f32[3,256,256]{2,0,1:T(4,128)}), f32[3,256,256]{2,0,1:T(4,128)S(1)}, u32[]{:S(2)}, u32[]{:S(2)}) async-start(f32[3,256,256]{2,0,1:T(4,128)} %copy.61), calls=%async_computation.1 | async-start | bytes 2097152 | tf_op jit(solution)/shard_map/all_to_all | solution.py:69
  62.0 2.9 %copy-start.5 = (bf16[3,1024,128]{2,1,0:T(8,128)(2,1)S(1)}, bf16[3,1024,128]{2,1,0:T(8,128)(2,1)}, u32[]{:S(2)}) copy-start(bf16[3,1024,128]{2,1,0:T(8,128)(2,1)} %param.15) | copy-start | bytes 2359300
  85.0 2.7 %copy-start.6 = (bf16[3,1024,128]{2,1,0:T(8,128)(2,1)S(1)}, bf16[3,1024,128]{2,1,0:T(8,128)(2,1)}, u32[]{:S(2)}) copy-start(bf16[3,1024,128]{2,1,0:T(8,128)(2,1)} %param.15) | copy-start | bytes 2359300
  86.2 9.0 %collective-permute-start = (f32[16,16,256]{2,0,1:T(8,128)S(1)}, f32[16,16,256]{2,0,1:T(8,128)S(1)}, u32[]{:S(2)}, u32[]{:S(2)}) collective-permute-start(f32[16,16,256]{2,0,1:T(8,128)S(1)} %slice.39), channel_id=1, source_target_pairs={{0,16},{16,0},{1,17},{17,1},{2,18},{18,2},{3,19},{19,3},{4,20},{20... | collective-permute-start | bytes 786440 | tf_op jit(solution)/shard_map/ppermute | solution.py:11
where the time goes:
time: 97.5 us; the launch traced here: 96.1 us
  local copies, waits for them, and re-layouts  33.3 us (34%)
  matrix products  22.8 us (23%)
  waiting for transfers between devices  22.2 us (23%)
  starting transfers between devices  15 us (15%)
  between operations  1.82 us (2%)
    dot_general x12, matrix products, contract(): lax.dot_general(left, right, (((0,), (0,)), ((), ())), preferred_element_...  17.6 us
    all_to_all x1, waiting for transfers between devices, per_device(): lax.all_to_all(parts, 'sub', split_axis=1, concat_axis=0, tiled=True)  17.5 us
    gather x9, local copies, waits for them, and re-layouts, per_device(): placed = reduced[inverse][:, inverse] * active  11 us
    all_to_all x1, starting transfers between devices, per_device(): lax.all_to_all(spread_hot, 'sub', split_axis=1, concat_axis=0, tiled=True)  7.46 us
    unnamed x27, local copies, waits for them, and re-layouts  6.7 us
    all_to_all x1, starting transfers between devices, per_device(): lax.all_to_all(parts, 'sub', split_axis=1, concat_axis=0, tiled=True)  5.96 us
    ppermute x1, waiting for transfers between devices, shifted(): lax.ppermute(value, axis, [(i, (i + by) % peers) for i in range(peers)])  4.76 us
    dot_general x3, local copies, waits for them, and re-layouts, contract(): lax.dot_general(left, right, (((0,), (0,)), ((), ())), preferred_element_...  4.45 us
  transfers between devices with their start and end apart: 3, of which 2 were waited for; matrix products, arithmetic and copies ran while one was open for 55% of the time, Pallas kernels for 0%

commit v1 on v0

v1 whole, which is shorter than its diff:
```python
import functools

import jax
import jax.numpy as jnp
from jax import lax
from jax.experimental import pallas as pl
from jax.experimental.pallas import tpu as pltpu
from jax.sharding import PartitionSpec as P

NBG = 16
ROWS = 8
MESH = pl.DeviceIdType.MESH


def split(value):
    high = value.astype(jnp.bfloat16)
    low = (value - high.astype(jnp.float32)).astype(jnp.bfloat16)
    return high, low


def dot(left, right, left_dim=1, right_dim=0):
    return lax.dot_general(
        left,
        right,
        (((left_dim,), (right_dim,)), ((), ())),
        preferred_element_type=jnp.float32,
    )


def send_order(peers):
    return sorted(range(1, peers), key=lambda step: (abs(step - peers // 2), step))


def kernel(
    n_grp,
    n_sub,
    counts,
    codes,
    perms,
    mass_ii,
    mass_ib,
    mass_bb,
    psi_in,
    phi_in,
    blocks,
    coupling,
    m_ii,
    m_ib,
    m_bb,
    psi,
    phi,
    product,
    placed,
    got,
    key_mine,
    key_got,
    hot,
    home,
    ahead,
    passed,
    in_sem,
    send_sem,
    got_sem,
    key_send_sem,
    key_sem,
    pass_send_sem,
    pass_sem,
):
    grp = lax.axis_index("grp")
    me = lax.axis_index("sub")
    slots, interior, width = psi.shape
    chunks = got.shape[0]
    own_rows = chunks * ROWS
    lanes = n_sub * ROWS
    after = lax.rem(grp + 1, n_grp)
    before = lax.rem(grp + n_grp - 1, n_grp)

    def loads(slot):
        pairs = ((psi_in, psi), (mass_ii, m_ii), (mass_ib, m_ib), (mass_bb, m_bb), (phi_in, phi))
        return [
            pltpu.make_async_copy(source.at[slot], held.at[slot], in_sem.at[slot, index])
            for index, (source, held) in enumerate(pairs)
        ]

    for copy in loads(0):
        copy.start()

    order = send_order(n_sub)
    peers = [lax.rem(me + step, n_sub) for step in order]
    barrier = pltpu.get_barrier_semaphore()
    for peer in peers:
        pl.semaphore_signal(barrier, inc=1, device_id=(grp, peer), device_id_type=MESH)
    pl.semaphore_signal(barrier, inc=1, device_id=(after, me), device_id_type=MESH)
    greeted = len(peers) + 1
    if n_grp > 2:
        pl.semaphore_signal(barrier, inc=1, device_id=(before, me), device_id_type=MESH)
        greeted += 1

    lane = lax.broadcasted_iota(jnp.int32, (1, lanes), 1)
    key_mine[...] = jnp.zeros_like(key_mine)
    for slot in range(slots):
        code = jnp.where(slot < counts[0], codes[slot] * ROWS, -2 * NBG * ROWS)
        key_mine[slot : slot + 1, :] = jnp.where(lane // ROWS == me, code + lane % ROWS, 0)
    key_got[pl.ds(me, 1)] = key_mine[...][None]

    def key_copy(peer):
        return pltpu.make_async_remote_copy(
            src_ref=key_mine,
            dst_ref=key_got.at[me],
            send_sem=key_send_sem,
            recv_sem=key_sem,
            device_id=(grp, peer),
            device_id_type=MESH,
        )

    @pl.loop(0, slots)
    def one_slot(slot):
        copies = loads(slot)

        @pl.when(slot + 1 < slots)
        def ahead_loads():
            for copy in loads(slot + 1):
                copy.start()

        copies[0].wait()
        copies[1].wait()
        modes = psi[slot]
        step = min(interior, 256)
        for top in range(0, interior, step):
            product[top : top + step, :] = dot(m_ii[slot, top : top + step, :], modes).astype(
                jnp.bfloat16
            )
        for copy in copies[2:]:
            copy.wait()
        mixed = m_ib[slot]
        made = product[...]
        reduced = dot(modes, made, 0, 0) + dot(modes, mixed, 0, 0) + dot(mixed, modes, 0, 0)
        reduced = reduced + m_bb[slot].astype(jnp.float32)
        place = lax.broadcasted_iota(jnp.int32, (width, width), 0)
        pick = jnp.where(place == perms[pl.ds(slot, 1), :], 1.0, 0.0).astype(jnp.bfloat16)
        high, low = split(reduced)
        high = dot(high, pick, 1, 1).astype(jnp.bfloat16)
        low = dot(low, pick, 1, 1).astype(jnp.bfloat16)
        placed[slot] = dot(pick, high) + dot(pick, low)
        active = jnp.where(slot < counts[0], 1.0, 0.0)
        fixed = phi[slot]
        coupling[slot] = (dot(fixed, made, 0, 0) + dot(fixed, mixed, 0, 0)) * active
        for chunk in range(chunks):
            mine = pl.multiple_of(me * own_rows + chunk * ROWS, ROWS)
            got[chunk, slot, pl.ds(me, 1)] = placed[slot, pl.ds(mine, ROWS), :][None]

        @pl.when(slot == 0)
        def enter():
            pl.semaphore_wait(barrier, greeted)
            for peer in peers:
                key_copy(peer).start()

        for chunk in range(chunks):
            for peer in peers:
                top = pl.multiple_of(peer * own_rows + chunk * ROWS, ROWS)
                pltpu.make_async_remote_copy(
                    src_ref=placed.at[slot, pl.ds(top, ROWS), :],
                    dst_ref=got.at[chunk, slot, me],
                    send_sem=send_sem.at[chunk, slot],
                    recv_sem=got_sem.at[chunk, slot],
                    device_id=(grp, peer),
                    device_id_type=MESH,
                ).start()

    many = n_sub - 1
    all_keys = key_got.at[pl.ds(0, many)]
    pltpu.make_async_copy(all_keys, all_keys, key_sem).wait()
    keys = jnp.sum(key_got[...], axis=0)
    target = lax.broadcasted_iota(jnp.int32, (2 * NBG * ROWS, lanes), 0)
    for slot in range(slots):
        hot[slot] = jnp.where(target == keys[slot : slot + 1, :], 1.0, 0.0).astype(jnp.bfloat16)

    def pass_copy(chunk):
        return pltpu.make_async_remote_copy(
            src_ref=ahead.at[chunk],
            dst_ref=passed.at[chunk],
            send_sem=pass_send_sem.at[chunk],
            recv_sem=pass_sem.at[chunk],
            device_id=(after, me),
            device_id_type=MESH,
        )

    for chunk in range(chunks):
        total = None
        for slot in range(slots):
            arrived = got.at[chunk, slot, pl.ds(0, many)]
            pltpu.make_async_copy(arrived, arrived, got_sem.at[chunk, slot]).wait()
            high, low = split(got[chunk, slot].reshape(lanes, width))
            part = dot(hot[slot], high) + dot(hot[slot], low)
            total = part if total is None else total + part
        ahead[chunk] = total[NBG * ROWS :]
        home[chunk] = total[: NBG * ROWS]
        pass_copy(chunk).start()

    for chunk in range(chunks):
        pass_copy(chunk).wait()
        own = home[chunk] + passed[chunk]
        blocks[:, chunk * ROWS : (chunk + 1) * ROWS, :] = own.reshape(NBG, ROWS, width)

    pltpu.make_async_copy(all_keys, all_keys, key_send_sem).wait()
    for chunk in range(chunks):
        for slot in range(slots):
            arrived = got.at[chunk, slot, pl.ds(0, many)]
            pltpu.make_async_copy(arrived, arrived, send_sem.at[chunk, slot]).wait()


def per_device(n_grp, n_sub, counts, block_map, perms, mass_ii, mass_ib, mass_bb, psi, phi):
    slots, interior, width = psi.shape
    modes = phi.shape[2]
    own_rows = width // n_sub
    chunks = own_rows // ROWS
    lanes = n_sub * ROWS
    key_rows = -(-slots // 8) * 8
    smem = pl.BlockSpec(memory_space=pltpu.SMEM)
    vmem = pl.BlockSpec(memory_space=pltpu.VMEM)
    hbm = pl.BlockSpec(memory_space=pl.ANY)
    bf16, f32, i32 = jnp.bfloat16, jnp.float32, jnp.int32
    dma = pltpu.SemaphoreType.DMA
    return pl.pallas_call(
        functools.partial(kernel, n_grp, n_sub),
        out_shape=(
            jax.ShapeDtypeStruct((NBG, own_rows, width), f32),
            jax.ShapeDtypeStruct((slots, modes, width), f32),
        ),
        in_specs=[smem, smem, vmem] + [hbm] * 5,
        out_specs=(vmem, vmem),
        scratch_shapes=[
            pltpu.VMEM(mass_ii.shape, bf16),
            pltpu.VMEM(mass_ib.shape, bf16),
            pltpu.VMEM(mass_bb.shape, bf16),
            pltpu.VMEM(psi.shape, bf16),
            pltpu.VMEM(phi.shape, bf16),
            pltpu.VMEM((interior, width), bf16),
            pltpu.VMEM((slots, width, width), f32),
            pltpu.VMEM((chunks, slots, n_sub, ROWS, width), f32),
            pltpu.VMEM((key_rows, lanes), i32),
            pltpu.VMEM((n_sub, key_rows, lanes), i32),
            pltpu.VMEM((slots, 2 * NBG * ROWS, lanes), bf16),
            pltpu.VMEM((chunks, NBG * ROWS, width), f32),
            pltpu.VMEM((chunks, NBG * ROWS, width), f32),
            pltpu.VMEM((chunks, NBG * ROWS, width), f32),
            dma((slots, 5)),
            dma((chunks, slots)),
            dma((chunks, slots)),
            dma,
            dma,
            dma((chunks,)),
            dma((chunks,)),
        ],
        compiler_params=pltpu.CompilerParams(
            collective_id=0, has_side_effects=True, vmem_limit_bytes=56 * 1024 * 1024
        ),
    )(counts, block_map, perms, mass_ii, mass_ib, mass_bb, psi, phi)


def solution(mesh):
    both = P(("grp", "sub"))
    return jax.shard_map(
        functools.partial(per_device, mesh.shape["grp"], mesh.shape["sub"]),
        mesh=mesh,
        in_specs=(both,) * 8,
        out_specs=(P("grp", "sub", None), both),
        check_vma=False,
    )
```

time: 97.5 us -> 41.5 us (0.43); the launches traced: 96.1 us -> 41.3 us
  Pallas kernels: 0 us -> 36.6 us
  local copies, waits for them, and re-layouts: 33.3 us -> 3.44 us
  matrix products: 22.8 us -> 0 us
  waiting for transfers between devices: 22.2 us -> 0 us
  starting transfers between devices: 15 us -> 0 us
    pallas_call x0 -> x1, Pallas kernels: none -> 36.6 us  [per_device(): pl.pallas_call(functools.partial(kernel, n_grp, n_sub), out_shape=(jax.Sh...]
    dot_general x16 -> x0, matrix products: 22.8 us -> none  [the longest x12 17.6 us: contract(): lax.dot_general(left, right, (((0,), (0,)), ((), ())), preferred_element_...]
    all_to_all x2 -> x0, waiting for transfers between devices: 17.5 us -> none  [the longest x1 17.5 us: per_device(): lax.all_to_all(parts, 'sub', split_axis=1, concat_axis=0, tiled=True)]
    all_to_all x2 -> x0, starting transfers between devices: 13.4 us -> none  [the longest x1 7.46 us: per_device(): lax.all_to_all(spread_hot, 'sub', split_axis=1, concat_axis=0, tiled=True)]
    gather x9 -> x0, local copies, waits for them, and re-layouts: 11 us -> none  [per_device(): placed = reduced[inverse][:, inverse] * active]
    ppermute x1 -> x0, waiting for transfers between devices: 4.76 us -> none  [shifted(): lax.ppermute(value, axis, [(i, (i + by) % peers) for i in range(peers)])]
    dot_general x3 -> x0, local copies, waits for them, and re-layouts: 4.45 us -> none  [contract(): lax.dot_general(left, right, (((0,), (0,)), ((), ())), preferred_element_...]
    scatter x3 -> x0, local copies, waits for them, and re-layouts: 4.19 us -> none  [per_device(): jnp.zeros((width,), jnp.int32).at[perm_row]]
  transfers between devices with their start and end apart: 3 -> 0, of which waited for: 2 -> 0; matrix products, arithmetic and copies ran while one was open for 55% -> 0% of each run, Pallas kernels for 0% -> 0%
where the time goes in v1:
time: 41.5 us; the launch traced here: 41.3 us
  Pallas kernels  36.6 us (88%)
  local copies, waits for them, and re-layouts  3.44 us (8%)
  between operations  1.29 us (3%)
    pallas_call x1, Pallas kernels, per_device(): pl.pallas_call(functools.partial(kernel, n_grp, n_sub), out_shape=(jax.Sh...  36.6 us
    unnamed x2, local copies, waits for them, and re-layouts  3.44 us

profile of v1, /device:TPU:0, one launch (start us, length us, event | category | flops | bytes accessed | tf_op | source)
XLA Modules:
  0.0 41.3 jit_solution(13871889988837124284)
XLA Ops:
  1.3 36.6 %shard_map.95 = (f32[16,16,256]{2,1,0:T(8,128)}, f32[3,128,256]{2,1,0:T(8,128)}) custom-call(s32[1]{0:T(128)S(6)} %copy.12.counts, s32[3]{0:T(128)} %codes.1, s32[3,256]{1,0:T(4,128)} %perms.1, bf16[3,1024,1024]{2,1,0:T(8,128)(2,1)} %mass_ii.1, bf16[3,1024,256]{2,1,0:T(8,128)(2,1)} %mass_ib.1, bf16[3,256,256]{2,1,0:T(8,128)(2,1)} %mass_bb.1, ...), custom_call_target="tpu_custom_call" | custom-call | tf_op jit(solution)/shard_map/pallas_call | solution.py:224
  37.9 1.7 %copy.13 = f32[16,16,256]{2,1,0:T(8,128)} copy(f32[16,16,256]{2,1,0:T(8,128)} %get-tuple-element.4) | data formatting | bytes 524288
  39.5 1.8 %copy.14 = f32[3,128,256]{2,1,0:T(8,128)} copy(f32[3,128,256]{2,1,0:T(8,128)} %get-tuple-element.5) | data formatting | bytes 786432

commit v2 on v1

--- a/solution.py
+++ b/solution.py
@@ -9,6 +9,8 @@
 
 NBG = 16
 ROWS = 8
+LANES = 128
+WINDOW = 2
 MESH = pl.DeviceIdType.MESH
 
 
@@ -55,8 +57,7 @@
     key_mine,
     key_got,
     hot,
-    home,
-    ahead,
+    sums,
     passed,
     in_sem,
     send_sem,
@@ -70,7 +71,8 @@
     me = lax.axis_index("sub")
     slots, interior, width = psi.shape
     chunks = got.shape[0]
-    own_rows = chunks * ROWS
+    cuts = width // LANES
+    own_rows = chunks // cuts * ROWS
     lanes = n_sub * ROWS
     after = lax.rem(grp + 1, n_grp)
     before = lax.rem(grp + n_grp - 1, n_grp)
@@ -112,6 +114,19 @@
             device_id=(grp, peer),
             device_id_type=MESH,
         )
+
+    def send(chunk, slot):
+        for peer in peers:
+            top = pl.multiple_of(peer * own_rows + chunk // cuts * ROWS, ROWS)
+            left = chunk % cuts * LANES
+            pltpu.make_async_remote_copy(
+                src_ref=placed.at[slot, pl.ds(top, ROWS), pl.ds(left, LANES)],
+                dst_ref=got.at[chunk, slot, me],
+                send_sem=send_sem.at[chunk, slot],
+                recv_sem=got_sem.at[chunk, slot],
+                device_id=(grp, peer),
+                device_id_type=MESH,
+            ).start()
 
     @pl.loop(0, slots)
     def one_slot(slot):
@@ -146,8 +161,10 @@
         fixed = phi[slot]
         coupling[slot] = (dot(fixed, made, 0, 0) + dot(fixed, mixed, 0, 0)) * active
         for chunk in range(chunks):
-            mine = pl.multiple_of(me * own_rows + chunk * ROWS, ROWS)
-            got[chunk, slot, pl.ds(me, 1)] = placed[slot, pl.ds(mine, ROWS), :][None]
+            mine = pl.multiple_of(me * own_rows + chunk // cuts * ROWS, ROWS)
+            left = chunk % cuts * LANES
+            own = placed[slot, pl.ds(mine, ROWS), left : left + LANES]
+            got[chunk, slot, pl.ds(me, 1)] = own[None]
 
         @pl.when(slot == 0)
         def enter():
@@ -155,17 +172,14 @@
             for peer in peers:
                 key_copy(peer).start()
 
-        for chunk in range(chunks):
-            for peer in peers:
-                top = pl.multiple_of(peer * own_rows + chunk * ROWS, ROWS)
-                pltpu.make_async_remote_copy(
-                    src_ref=placed.at[slot, pl.ds(top, ROWS), :],
-                    dst_ref=got.at[chunk, slot, me],
-                    send_sem=send_sem.at[chunk, slot],
-                    recv_sem=got_sem.at[chunk, slot],
-                    device_id=(grp, peer),
-                    device_id_type=MESH,
-                ).start()
+        @pl.when(slot < slots - 1)
+        def spread():
+            for chunk in range(chunks):
+                send(chunk, slot)
+
+    window = min(WINDOW, chunks)
+    for chunk in range(window):
+        send(chunk, slots - 1)
 
     many = n_sub - 1
     all_keys = key_got.at[pl.ds(0, many)]
@@ -177,7 +191,7 @@
 
     def pass_copy(chunk):
         return pltpu.make_async_remote_copy(
-            src_ref=ahead.at[chunk],
+            src_ref=sums.at[chunk, pl.ds(NBG * ROWS, NBG * ROWS)],
             dst_ref=passed.at[chunk],
             send_sem=pass_send_sem.at[chunk],
             recv_sem=pass_sem.at[chunk],
@@ -185,22 +199,28 @@
             device_id_type=MESH,
         )
 
-    for chunk in range(chunks):
-        total = None
-        for slot in range(slots):
-            arrived = got.at[chunk, slot, pl.ds(0, many)]
-            pltpu.make_async_copy(arrived, arrived, got_sem.at[chunk, slot]).wait()
-            high, low = split(got[chunk, slot].reshape(lanes, width))
-            part = dot(hot[slot], high) + dot(hot[slot], low)
-            total = part if total is None else total + part
-        ahead[chunk] = total[NBG * ROWS :]
-        home[chunk] = total[: NBG * ROWS]
-        pass_copy(chunk).start()
+    def owner_sum(chunk, slot):
+        arrived = got.at[chunk, slot, pl.ds(0, many)]
+        pltpu.make_async_copy(arrived, arrived, got_sem.at[chunk, slot]).wait()
+        high, low = split(got[chunk, slot].reshape(lanes, LANES))
+        return dot(hot[slot], high) + dot(hot[slot], low)
+
+    for slot in range(slots):
+        for chunk in range(chunks):
+            total = owner_sum(chunk, slot)
+            if slot > 0:
+                total = total + sums[chunk]
+            sums[chunk] = total
+            if slot == slots - 1:
+                pass_copy(chunk).start()
+                if chunk + window < chunks:
+                    send(chunk + window, slot)
 
     for chunk in range(chunks):
         pass_copy(chunk).wait()
-        own = home[chunk] + passed[chunk]
-        blocks[:, chunk * ROWS : (chunk + 1) * ROWS, :] = own.reshape(NBG, ROWS, width)
+        own = sums[chunk, : NBG * ROWS] + passed[chunk]
+        top, left = chunk // cuts * ROWS, chunk % cuts * LANES
+        blocks[:, top : top + ROWS, left : left + LANES] = own.reshape(NBG, ROWS, LANES)
 
     pltpu.make_async_copy(all_keys, all_keys, key_send_sem).wait()
     for chunk in range(chunks):
@@ -209,12 +229,215 @@
             pltpu.make_async_copy(arrived, arrived, send_sem.at[chunk, slot]).wait()
 
 
+def halves_kernel(
+    n_grp,
+    n_sub,
+    counts,
+    codes,
+    perms,
+    mass_ii,
+    mass_ib,
+    mass_bb,
+    psi_in,
+    phi_in,
+    blocks,
+    coupling,
+    m_ii,
+    m_ib,
+    m_bb,
+    psi,
+    phi,
+    product,
+    placed,
+    got,
+    key_mine,
+    key_got,
+    hot,
+    sums,
+    passed,
+    in_sem,
+    send_sem,
+    got_sem,
+    key_send_sem,
+    key_sem,
+    pass_send_sem,
+    pass_sem,
+):
+    grp = lax.axis_index("grp")
+    me = lax.axis_index("sub")
+    slots, interior, width = psi.shape
+    own_rows = width // n_sub
+    half = n_sub // 2
+    lanes = n_sub * ROWS
+    part_rows = NBG * ROWS
+    other = 1 - grp
+    far = lax.rem(me + half, n_sub)
+    member = grp * half + lax.rem(me, half)
+    first = me - lax.rem(me, half)
+
+    def loads(slot):
+        pairs = ((psi_in, psi), (mass_ii, m_ii), (mass_ib, m_ib), (mass_bb, m_bb), (phi_in, phi))
+        return [
+            pltpu.make_async_copy(source.at[slot], held.at[slot], in_sem.at[slot, index])
+            for index, (source, held) in enumerate(pairs)
+        ]
+
+    for copy in loads(0):
+        copy.start()
+
+    peers = []
+    for step in send_order(n_sub):
+        index = lax.rem(member + step, n_sub)
+        peers.append((index // half, first + lax.rem(index, half)))
+    barrier = pltpu.get_barrier_semaphore()
+    for peer in peers + [(grp, far), (other, far)]:
+        pl.semaphore_signal(barrier, inc=1, device_id=peer, device_id_type=MESH)
+    greeted = len(peers) + 2
+
+    lane = lax.broadcasted_iota(jnp.int32, (1, lanes), 1)
+    key_mine[...] = jnp.zeros_like(key_mine)
+    for slot in range(slots):
+        code = codes[slot]
+        block = lax.rem(grp + code // NBG, n_grp) * NBG + lax.rem(code, NBG)
+        block = jnp.where(slot < counts[0], block, -n_grp * NBG) * ROWS
+        key_mine[slot : slot + 1, :] = jnp.where(lane // ROWS == member, block + lane % ROWS, 0)
+    key_got[pl.ds(member, 1)] = key_mine[...][None]
+
+    def key_copy(peer):
+        return pltpu.make_async_remote_copy(
+            src_ref=key_mine,
+            dst_ref=key_got.at[member],
+            send_sem=key_send_sem,
+            recv_sem=key_sem,
+            device_id=peer,
+            device_id_type=MESH,
+        )
+
+    def row_of(part, peer):
+        owner = lax.rem(peer[1] + half, n_sub) if part == 0 else peer[1]
+        return pl.multiple_of(owner * own_rows + peer[0] * ROWS, ROWS)
+
+    def send(part, slot):
+        for peer in peers:
+            pltpu.make_async_remote_copy(
+                src_ref=placed.at[slot, pl.ds(row_of(part, peer), ROWS), :],
+                dst_ref=got.at[part, slot, member],
+                send_sem=send_sem.at[part, slot],
+                recv_sem=got_sem.at[part, slot],
+                device_id=peer,
+                device_id_type=MESH,
+            ).start()
+
+    @pl.loop(0, slots)
+    def one_slot(slot):
+        copies = loads(slot)
+
+        @pl.when(slot + 1 < slots)
+        def ahead_loads():
+            for copy in loads(slot + 1):
+                copy.start()
+
+        copies[0].wait()
+        copies[1].wait()
+        modes = psi[slot]
+        step = min(interior, 256)
+        for top in range(0, interior, step):
+            product[top : top + step, :] = dot(m_ii[slot, top : top + step, :], modes).astype(
+                jnp.bfloat16
+            )
+        for copy in copies[2:]:
+            copy.wait()
+        mixed = m_ib[slot]
+        made = product[...]
+        reduced = dot(modes, made, 0, 0) + dot(modes, mixed, 0, 0) + dot(mixed, modes, 0, 0)
+        reduced = reduced + m_bb[slot].astype(jnp.float32)
+        place = lax.broadcasted_iota(jnp.int32, (width, width), 0)
+        pick = jnp.where(place == perms[pl.ds(slot, 1), :], 1.0, 0.0).astype(jnp.bfloat16)
+        high, low = split(reduced)
+        high = dot(high, pick, 1, 1).astype(jnp.bfloat16)
+        low = dot(low, pick, 1, 1).astype(jnp.bfloat16)
+        placed[slot] = dot(pick, high) + dot(pick, low)
+        active = jnp.where(slot < counts[0], 1.0, 0.0)
+        fixed = phi[slot]
+        coupling[slot] = (dot(fixed, made, 0, 0) + dot(fixed, mixed, 0, 0)) * active
+        for part in range(2):
+            own = placed[slot, pl.ds(row_of(part, (grp, me)), ROWS), :]
+            got[part, slot, pl.ds(member, 1)] = own[None]
+
+        @pl.when(slot == 0)
+        def enter():
+            pl.semaphore_wait(barrier, greeted)
+            for peer in peers:
+                key_copy(peer).start()
+
+        send(0, slot)
+
+    for slot in range(slots):
+        send(1, slot)
+
+    many = n_sub - 1
+    all_keys = key_got.at[pl.ds(0, many)]
+    pltpu.make_async_copy(all_keys, all_keys, key_sem).wait()
+    keys = jnp.sum(key_got[...], axis=0)
+    target = lax.broadcasted_iota(jnp.int32, (2 * NBG * ROWS, lanes), 0)
+    for slot in range(slots):
+        hot[slot] = jnp.where(target == keys[slot : slot + 1, :], 1.0, 0.0).astype(jnp.bfloat16)
+
+    def pass_copy(source, part, place, peer):
+        return pltpu.make_async_remote_copy(
+            src_ref=sums.at[source, pl.ds(pl.multiple_of(part * part_rows, part_rows), part_rows)],
+            dst_ref=passed.at[place],
+            send_sem=pass_send_sem.at[source],
+            recv_sem=pass_sem.at[place],
+            device_id=peer,
+            device_id_type=MESH,
+        )
+
+    def owner_sum(part):
+        total = None
+        for slot in range(slots):
+            arrived = got.at[part, slot, pl.ds(0, many)]
+            pltpu.make_async_copy(arrived, arrived, got_sem.at[part, slot]).wait()
+            high, low = split(got[part, slot].reshape(lanes, width))
+            one = dot(hot[slot], high) + dot(hot[slot], low)
+            total = one if total is None else total + one
+        sums[part] = total
+
+    owner_sum(0)
+    pass_copy(0, other, grp, (other, far)).start()
+    pass_copy(0, grp, grp, (grp, far)).start()
+    owner_sum(1)
+    pass_copy(1, other, 2, (other, me)).start()
+
+    pltpu.make_async_copy(all_keys, all_keys, key_send_sem).wait()
+    for part in range(2):
+        for slot in range(slots):
+            arrived = got.at[part, slot, pl.ds(0, many)]
+            pltpu.make_async_copy(arrived, arrived, send_sem.at[part, slot]).wait()
+
+    for place in range(3):
+        pltpu.make_async_copy(passed.at[place], passed.at[place], pass_sem.at[place]).wait()
+    kept = sums[1, pl.ds(pl.multiple_of(grp * part_rows, part_rows), part_rows), :]
+    for row, near in ((grp, kept), (other, passed[2])):
+        value = (passed[row] + near).reshape(NBG, ROWS, width)
+        blocks[:, pl.ds(pl.multiple_of(row * ROWS, ROWS), ROWS), :] = value
+
+    both = sums.at[0]
+    pltpu.make_async_copy(both, both, pass_send_sem.at[0]).wait()
+    pltpu.make_async_copy(passed.at[2], passed.at[2], pass_send_sem.at[1]).wait()
+
+
 def per_device(n_grp, n_sub, counts, block_map, perms, mass_ii, mass_ib, mass_bb, psi, phi):
     slots, interior, width = psi.shape
     modes = phi.shape[2]
     own_rows = width // n_sub
-    chunks = own_rows // ROWS
+    chunks = own_rows // ROWS * (width // LANES)
+    cut = LANES
     lanes = n_sub * ROWS
+    body = kernel
+    places = chunks
+    if n_grp == 2 and own_rows == 2 * ROWS and n_sub % 2 == 0:
+        body, chunks, places, cut = halves_kernel, 2, 3, width
     key_rows = -(-slots // 8) * 8
     smem = pl.BlockSpec(memory_space=pltpu.SMEM)
     vmem = pl.BlockSpec(memory_space=pltpu.VMEM)
@@ -222,10 +445,10 @@
     bf16, f32, i32 = jnp.bfloat16, jnp.float32, jnp.int32
     dma = pltpu.SemaphoreType.DMA
     return pl.pallas_call(
-        functools.partial(kernel, n_grp, n_sub),
+        functools.partial(body, n_grp, n_sub),
         out_shape=(
-            jax.ShapeDtypeStruct((NBG, own_rows, width), f32),
-            jax.ShapeDtypeStruct((slots, modes, width), f32),
+            pltpu.VMEM((NBG, own_rows, width), f32),
+            pltpu.VMEM((slots, modes, width), f32),
         ),
         in_specs=[smem, smem, vmem] + [hbm] * 5,
         out_specs=(vmem, vmem),
@@ -237,20 +460,19 @@
             pltpu.VMEM(phi.shape, bf16),
             pltpu.VMEM((interior, width), bf16),
             pltpu.VMEM((slots, width, width), f32),
-            pltpu.VMEM((chunks, slots, n_sub, ROWS, width), f32),
+            pltpu.VMEM((chunks, slots, n_sub, ROWS, cut), f32),
             pltpu.VMEM((key_rows, lanes), i32),
             pltpu.VMEM((n_sub, key_rows, lanes), i32),
             pltpu.VMEM((slots, 2 * NBG * ROWS, lanes), bf16),
-            pltpu.VMEM((chunks, NBG * ROWS, width), f32),
-            pltpu.VMEM((chunks, NBG * ROWS, width), f32),
-            pltpu.VMEM((chunks, NBG * ROWS, width), f32),
+            pltpu.VMEM((chunks, 2 * NBG * ROWS, cut), f32),
+            pltpu.VMEM((places, NBG * ROWS, cut), f32),
             dma((slots, 5)),
             dma((chunks, slots)),
             dma((chunks, slots)),
             dma,
             dma,
             dma((chunks,)),
-            dma((chunks,)),
+            dma((places,)),
         ],
         compiler_params=pltpu.CompilerParams(
             collective_id=0, has_side_effects=True, vmem_limit_bytes=56 * 1024 * 1024

time: 41.5 us -> 36.2 us (0.87)
  Pallas kernels: 36.6 us -> 33.2 us
  local copies, waits for them, and re-layouts: 3.44 us -> 1.45 us
    pallas_call x1, Pallas kernels: 36.6 us -> 33.2 us  [per_device(): pl.pallas_call(functools.partial(body, n_grp, n_sub), out_shape=(pltpu.VM...]
    unnamed x2, local copies, waits for them, and re-layouts: 3.44 us -> 1.45 us
where the time goes in v2:
time: 36.2 us; the launch traced here: 36 us
  Pallas kernels  33.2 us (92%)
  local copies, waits for them, and re-layouts  1.45 us (4%)
  between operations  1.29 us (4%)
    pallas_call x1, Pallas kernels, per_device(): pl.pallas_call(functools.partial(body, n_grp, n_sub), out_shape=(pltpu.VM...  33.2 us
    unnamed x2, local copies, waits for them, and re-layouts  1.45 us

profile of v2, /device:TPU:0, one launch (start us, length us, event | category | flops | bytes accessed | tf_op | source)
XLA Modules:
  0.0 36.0 jit_solution(7753475219876758716)
XLA Ops:
  1.3 33.2 %shard_map.95 = (f32[16,16,256]{2,1,0:T(8,128)S(1)}, f32[3,128,256]{2,1,0:T(8,128)S(1)}) custom-call(s32[1]{0:T(128)S(6)} %copy.14.counts, s32[3]{0:T(128)} %codes.1, s32[3,256]{1,0:T(4,128)} %perms.1, bf16[3,1024,1024]{2,1,0:T(8,128)(2,1)} %mass_ii.1, bf16[3,1024,256]{2,1,0:T(8,128)(2,1)} %mass_ib.1, bf16[3,256,256]{2,1,0:T(8,128)(2,1)} %mass_bb.1, ...), custom_call_target="tpu_custom_call" | custom-call | tf_op jit(solution)/shard_map/pallas_call | solution.py:447
  34.5 0.7 %copy.12 = f32[16,16,256]{2,1,0:T(8,128)} copy(f32[16,16,256]{2,1,0:T(8,128)S(1)} %get-tuple-element.2) | data formatting | bytes 524288
  35.2 0.7 %copy.13 = f32[3,128,256]{2,1,0:T(8,128)} copy(f32[3,128,256]{2,1,0:T(8,128)S(1)} %get-tuple-element.3) | data formatting | bytes 786432

commit v3 on v2

--- a/solution.py
+++ b/solution.py
@@ -47,11 +47,9 @@
     blocks,
     coupling,
     m_ii,
-    m_ib,
     m_bb,
-    psi,
-    phi,
-    product,
+    lhs,
+    rhs,
     placed,
     got,
     key_mine,
@@ -69,7 +67,7 @@
 ):
     grp = lax.axis_index("grp")
     me = lax.axis_index("sub")
-    slots, interior, width = psi.shape
+    slots, interior, width = psi_in.shape
     chunks = got.shape[0]
     cuts = width // LANES
     own_rows = chunks // cuts * ROWS
@@ -78,9 +76,15 @@
     before = lax.rem(grp + n_grp - 1, n_grp)
 
     def loads(slot):
-        pairs = ((psi_in, psi), (mass_ii, m_ii), (mass_ib, m_ib), (mass_bb, m_bb), (phi_in, phi))
+        pairs = (
+            (psi_in, lhs.at[slot, :, pl.ds(0, width)]),
+            (mass_ii, m_ii.at[slot]),
+            (mass_ib, rhs.at[slot, :, pl.ds(width, width)]),
+            (mass_bb, m_bb.at[slot]),
+            (phi_in, lhs.at[slot, :, pl.ds(width, lhs.shape[2] - width)]),
+        )
         return [
-            pltpu.make_async_copy(source.at[slot], held.at[slot], in_sem.at[slot, index])
+            pltpu.make_async_copy(source.at[slot], held, in_sem.at[slot, index])
             for index, (source, held) in enumerate(pairs)
         ]
 
@@ -139,27 +143,26 @@
 
         copies[0].wait()
         copies[1].wait()
-        modes = psi[slot]
         step = min(interior, 256)
+        modes = lhs[slot, :, :width]
         for top in range(0, interior, step):
-            product[top : top + step, :] = dot(m_ii[slot, top : top + step, :], modes).astype(
-                jnp.bfloat16
-            )
+            made = dot(m_ii[slot, top : top + step, :], modes).astype(jnp.bfloat16)
+            rhs[slot, top : top + step, :width] = made
         for copy in copies[2:]:
             copy.wait()
-        mixed = m_ib[slot]
-        made = product[...]
-        reduced = dot(modes, made, 0, 0) + dot(modes, mixed, 0, 0) + dot(mixed, modes, 0, 0)
-        reduced = reduced + m_bb[slot].astype(jnp.float32)
+        every = dot(lhs[slot], rhs[slot], 0, 0)
+        cross = every[:width, width:]
+        direct = every[:width, :width] + cross + m_bb[slot].astype(jnp.float32)
         place = lax.broadcasted_iota(jnp.int32, (width, width), 0)
         pick = jnp.where(place == perms[pl.ds(slot, 1), :], 1.0, 0.0).astype(jnp.bfloat16)
-        high, low = split(reduced)
-        high = dot(high, pick, 1, 1).astype(jnp.bfloat16)
-        low = dot(low, pick, 1, 1).astype(jnp.bfloat16)
-        placed[slot] = dot(pick, high) + dot(pick, low)
+        high, low = split(direct)
+        cross_high, cross_low = split(cross)
+        rows = dot(pick, high) + dot(pick, low)
+        rows = rows + dot(pick, cross_high, 1, 1) + dot(pick, cross_low, 1, 1)
+        high, low = split(rows)
+        placed[slot] = dot(high, pick, 1, 1) + dot(low, pick, 1, 1)
         active = jnp.where(slot < counts[0], 1.0, 0.0)
-        fixed = phi[slot]
-        coupling[slot] = (dot(fixed, made, 0, 0) + dot(fixed, mixed, 0, 0)) * active
+        coupling[slot] = (every[width:, :width] + every[width:, width:]) * active
         for chunk in range(chunks):
             mine = pl.multiple_of(me * own_rows + chunk // cuts * ROWS, ROWS)
             left = chunk % cuts * LANES
@@ -243,11 +246,9 @@
     blocks,
     coupling,
     m_ii,
-    m_ib,
     m_bb,
-    psi,
-    phi,
-    product,
+    lhs,
+    rhs,
     placed,
     got,
     key_mine,
@@ -265,7 +266,7 @@
 ):
     grp = lax.axis_index("grp")
     me = lax.axis_index("sub")
-    slots, interior, width = psi.shape
+    slots, interior, width = psi_in.shape
     own_rows = width // n_sub
     half = n_sub // 2
     lanes = n_sub * ROWS
@@ -276,9 +277,15 @@
     first = me - lax.rem(me, half)
 
     def loads(slot):
-        pairs = ((psi_in, psi), (mass_ii, m_ii), (mass_ib, m_ib), (mass_bb, m_bb), (phi_in, phi))
+        pairs = (
+            (psi_in, lhs.at[slot, :, pl.ds(0, width)]),
+            (mass_ii, m_ii.at[slot]),
+            (mass_ib, rhs.at[slot, :, pl.ds(width, width)]),
+            (mass_bb, m_bb.at[slot]),
+            (phi_in, lhs.at[slot, :, pl.ds(width, lhs.shape[2] - width)]),
+        )
         return [
-            pltpu.make_async_copy(source.at[slot], held.at[slot], in_sem.at[slot, index])
+            pltpu.make_async_copy(source.at[slot], held, in_sem.at[slot, index])
             for index, (source, held) in enumerate(pairs)
         ]
 
@@ -339,27 +346,26 @@
 
         copies[0].wait()
         copies[1].wait()
-        modes = psi[slot]
         step = min(interior, 256)
+        modes = lhs[slot, :, :width]
         for top in range(0, interior, step):
-            product[top : top + step, :] = dot(m_ii[slot, top : top + step, :], modes).astype(
-                jnp.bfloat16
-            )
+            made = dot(m_ii[slot, top : top + step, :], modes).astype(jnp.bfloat16)
+            rhs[slot, top : top + step, :width] = made
         for copy in copies[2:]:
             copy.wait()
-        mixed = m_ib[slot]
-        made = product[...]
-        reduced = dot(modes, made, 0, 0) + dot(modes, mixed, 0, 0) + dot(mixed, modes, 0, 0)
-        reduced = reduced + m_bb[slot].astype(jnp.float32)
+        every = dot(lhs[slot], rhs[slot], 0, 0)
+        cross = every[:width, width:]
+        direct = every[:width, :width] + cross + m_bb[slot].astype(jnp.float32)
         place = lax.broadcasted_iota(jnp.int32, (width, width), 0)
         pick = jnp.where(place == perms[pl.ds(slot, 1), :], 1.0, 0.0).astype(jnp.bfloat16)
-        high, low = split(reduced)
-        high = dot(high, pick, 1, 1).astype(jnp.bfloat16)
-        low = dot(low, pick, 1, 1).astype(jnp.bfloat16)
-        placed[slot] = dot(pick, high) + dot(pick, low)
+        high, low = split(direct)
+        cross_high, cross_low = split(cross)
+        rows = dot(pick, high) + dot(pick, low)
+        rows = rows + dot(pick, cross_high, 1, 1) + dot(pick, cross_low, 1, 1)
+        high, low = split(rows)
+        placed[slot] = dot(high, pick, 1, 1) + dot(low, pick, 1, 1)
         active = jnp.where(slot < counts[0], 1.0, 0.0)
-        fixed = phi[slot]
-        coupling[slot] = (dot(fixed, made, 0, 0) + dot(fixed, mixed, 0, 0)) * active
+        coupling[slot] = (every[width:, :width] + every[width:, width:]) * active
         for part in range(2):
             own = placed[slot, pl.ds(row_of(part, (grp, me)), ROWS), :]
             got[part, slot, pl.ds(member, 1)] = own[None]
@@ -454,11 +460,9 @@
         out_specs=(vmem, vmem),
         scratch_shapes=[
             pltpu.VMEM(mass_ii.shape, bf16),
-            pltpu.VMEM(mass_ib.shape, bf16),
             pltpu.VMEM(mass_bb.shape, bf16),
-            pltpu.VMEM(psi.shape, bf16),
-            pltpu.VMEM(phi.shape, bf16),
-            pltpu.VMEM((interior, width), bf16),
+            pltpu.VMEM((slots, interior, width + modes), bf16),
+            pltpu.VMEM((slots, interior, 2 * width), bf16),
             pltpu.VMEM((slots, width, width), f32),
             pltpu.VMEM((chunks, slots, n_sub, ROWS, cut), f32),
             pltpu.VMEM((key_rows, lanes), i32),

time: 36.2 us -> 34.7 us (0.959)
  Pallas kernels: 33.2 us -> 31.8 us
    pallas_call x1, Pallas kernels: 33.2 us -> 31.8 us  [per_device(): pl.pallas_call(functools.partial(body, n_grp, n_sub), out_shape=(pltpu.VM...]
where the time goes in v3:
time: 34.7 us; the launch traced here: 34.5 us
  Pallas kernels  31.8 us (92%)
  local copies, waits for them, and re-layouts  1.45 us (4%)
  between operations  1.29 us (4%)
    pallas_call x1, Pallas kernels, per_device(): pl.pallas_call(functools.partial(body, n_grp, n_sub), out_shape=(pltpu.VM...  31.8 us
    unnamed x2, local copies, waits for them, and re-layouts  1.45 us

profile of v3, /device:TPU:0, one launch (start us, length us, event | category | flops | bytes accessed | tf_op | source)
XLA Modules:
  0.0 34.5 jit_solution(5465119766254771218)
XLA Ops:
  1.3 31.8 %shard_map.95 = (f32[16,16,256]{2,1,0:T(8,128)S(1)}, f32[3,128,256]{2,1,0:T(8,128)S(1)}) custom-call(s32[1]{0:T(128)S(6)} %copy.14.counts, s32[3]{0:T(128)} %codes.1, s32[3,256]{1,0:T(4,128)} %perms.1, bf16[3,1024,1024]{2,1,0:T(8,128)(2,1)} %mass_ii.1, bf16[3,1024,256]{2,1,0:T(8,128)(2,1)} %mass_ib.1, bf16[3,256,256]{2,1,0:T(8,128)(2,1)} %mass_bb.1, ...), custom_call_target="tpu_custom_call" | custom-call | tf_op jit(solution)/shard_map/pallas_call | solution.py:453
  33.0 0.7 %copy.12 = f32[16,16,256]{2,1,0:T(8,128)} copy(f32[16,16,256]{2,1,0:T(8,128)S(1)} %get-tuple-element.2) | data formatting | bytes 524288
  33.8 0.7 %copy.13 = f32[3,128,256]{2,1,0:T(8,128)} copy(f32[3,128,256]{2,1,0:T(8,128)S(1)} %get-tuple-element.3) | data formatting | bytes 786432
